TPU v7x, 32 devices: a whole 2x2x4 slice. The times are simulated.
32 devices in a mesh: row: 8 (over z, x), col: 4 (over y, core).
Axes of the slice: x: 2, y: 2, z: 4, core: 2. Of those that a mesh axis runs over, the one named last changes fastest.
Arguments:
- basis_blocks: float32 [8, 16, 262144], P(None, None, ('col', 'row')), may hold values from -6 to 6
- tile_values: bfloat16 [4, 8, 384, 128, 128], P('col', 'row'), may hold values from -0.375 to 0.375
- tile_rows: int32 [4, 8, 384], P('col', 'row'), may hold values from 0 to 511
- tile_column: int32 [4, 8, 384], P('col', 'row'), may hold values from 0 to 255
- tile_count: int32 [4, 8], P('col', 'row'), may hold values from 1 to 384, as said below
- diagonal: float32 [262144], P(('col', 'row')), may hold values from 1 to 6
Outputs:
- new_block: float32 [16, 262144], P(None, ('col', 'row'))
- coefficients: float32 [8, 16, 16], replicated
- triangle: float32 [16, 16], replicated
Inputs may be any that keep to these rules, and one draw needn't show every extreme that they name: Each operator block stores tile_count tiles in its first slots; at most 384, and some block has exactly 384 in every draw. Slots past the count hold arbitrary data and are ignored.
All inputs are finite; a program needn't handle non-finite values.
Results may differ from a plain program's by a relative error of at most 0.0031.
Values may be sent and summed in bfloat16 or wider, within the bound.
A program may use at most 128 MiB of HBM per device.

v0:
```python
import jax
import jax.numpy as jnp
from jax import lax
from jax.sharding import PartitionSpec as P


def local(basis_blocks, tile_values, tile_rows, tile_column, tile_count, diagonal):
    rhs_width = basis_blocks.shape[1]
    seg_rows = basis_blocks.shape[2]
    total_rows = seg_rows * lax.axis_size("row") * lax.axis_size("col")
    block_tiles = lax.axis_size("row") * seg_rows // 128
    vector = basis_blocks[-1].astype(jnp.bfloat16)
    expanded = lax.all_gather(vector, "col", axis=1, tiled=True)
    xblocks = expanded.reshape(rhs_width, -1, 128)
    values = tile_values[0, 0]
    row_ids = tile_rows[0, 0]
    column_ids = tile_column[0, 0]
    live_count = tile_count[0, 0]
    live_tiles = jnp.arange(values.shape[0], dtype=jnp.int32) < live_count
    gathered = jnp.take(xblocks, column_ids, axis=1)
    products = jnp.einsum("stj,tji->tsi", gathered, values, preferred_element_type=jnp.float32)
    inside = live_tiles & (row_ids >= 0) & (row_ids < 0 + block_tiles)
    segment_ids = jnp.where(inside, row_ids - 0, block_tiles)
    summed = jax.ops.segment_sum(products, segment_ids, num_segments=block_tiles + 1)
    folded = lax.psum_scatter(summed[:block_tiles], "row", scatter_dimension=0, tiled=True)
    image_rows = folded.transpose(1, 0, 2).reshape(rhs_width, seg_rows)
    image_rows = image_rows + diagonal[None, :] * basis_blocks[-1]
    highest = lax.Precision.HIGHEST
    local_proj = jnp.einsum("kap,bp->kab", basis_blocks, image_rows, precision=highest)
    local_self = jnp.dot(image_rows, image_rows.T, precision=highest)
    local_basis = jnp.einsum("kap,lcp->kalc", basis_blocks, basis_blocks, precision=highest)
    proj_sum, image_sum, basis_sum = lax.psum((local_proj, local_self, local_basis), ("row", "col"))
    coefficients = proj_sum / total_rows
    image_gram = image_sum / total_rows
    basis_gram = basis_sum / total_rows
    projected = image_rows - jnp.einsum(
        "kab,kap->bp", coefficients, basis_blocks, precision=highest
    )
    cross_term = jnp.einsum("kab,kad->bd", coefficients, coefficients, precision=highest)
    basis_term = jnp.einsum(
        "kab,kalc,lcd->bd", coefficients, basis_gram, coefficients, precision=highest
    )
    gram_matrix = image_gram - 2.0 * cross_term + basis_term
    lower_factor = jnp.linalg.cholesky(gram_matrix)
    new_block = lax.linalg.triangular_solve(lower_factor, projected, left_side=True, lower=True)
    return (new_block, coefficients, lower_factor.T)


def solution(mesh):
    in_specs = (
        P(None, None, ("col", "row")),
        P("col", "row", None, None, None),
        P("col", "row", None),
        P("col", "row", None),
        P("col", "row"),
        P(("col", "row")),
    )
    out_specs = (P(None, ("col", "row")), P(), P())
    return jax.shard_map(local, mesh=mesh, in_specs=in_specs, out_specs=out_specs, check_vma=False)
```

profile of v0, /device:TPU:0, one launch (start us, length us, event | category | flops | bytes accessed | tf_op | source)
XLA Modules:
  0.0 285.5 jit_solution(4340497072909810050)
XLA Ops:
  8.0 0.0 all-gather.2.cloned.1.call-start
  8.0 1.8 bitcast_convert_fusion
  9.8 0.0 all-gather.2.cloned.1.call-update
  9.8 0.0 reduce-scatter.2.cloned.1.call-start
  10.5 0.7 reduce.7
  11.2 0.7 fusion.22
  11.9 0.7 fusion.23
  12.7 17.7 %all-gather.2.cloned.1.call-done = bf16[16,32768]{1,0:T(8,128)(2,1)} async-done(((bf16[16,8192]{1,0:T(8,128)(2,1)}), bf16[16,32768]{1,0:T(8,128)(2,1)}) %all-gather.2.cloned.1.call-update) | async-done | bytes 1048592 | tf_op jit(solution)/shard_map/all_gather | solution.py:13
  30.4 1.4 copy_bitcast_fusion
  31.8 2.6 gather_fusion
  34.4 6.9 %fusion = f32[384,16,128]{2,1,0:T(8,128)S(1)} fusion(bf16[1,1,384,128,128]{4,3,2,1,0:T(8,128)(2,1)} %param.7, bf16[384,16,128]{2,1,0:T(8,128)(2,1)} %gather_fusion, pred[384]{0:T(512)(128)(4,1)S(1)} %compare_and_fusion), kind=kOutput, calls=%fused_computation.2 | convolution fusion | flops 202113024 | bytes 17301888 | tf_op jit(solution)/shard_map/stj,tji->tsi/dot_general | solution.py:21
  41.2 2.2 broadcast_in_dim.19
  43.5 51.1 %scatter_fusion = f32[513,16,128]{2,1,0:T(8,128)} fusion(f32[513,16,128]{2,1,0:T(8,128)} %broadcast_in_dim.19, s32[384]{0:T(512)S(1)} %fusion.23, f32[384,16,128]{2,1,0:T(8,128)S(1)} %fusion), kind=kCustom, calls=%fused_computation.1 | custom fusion | flops 786432 | bytes 9438720 | tf_op jit(solution)/shard_map/scatter-add | solution.py:24
  94.6 4.4 %slice.21 = f32[512,16,128]{2,1,0:T(8,128)} slice(f32[513,16,128]{2,1,0:T(8,128)} %scatter_fusion), slice={[0:512], [0:16], [0:128]} | slice | bytes 8388608 | tf_op jit(solution)/shard_map/slice | solution.py:25
  99.0 0.0 reduce-scatter.2.cloned.1.call-update
  99.0 0.0 copy-start.1
  99.0 0.2 all-reduce.3.cloned.1.call-start
  99.3 18.0 %fusion.3 = f32[8,16,8,16]{3,1,2,0:T(8,128)} fusion(f32[8,16,8192]{2,1,0:T(8,128)} %param.6), kind=kOutput, calls=%fused_computation.6 | convolution fusion | flops 1610612736 | bytes 4259840 | tf_op jit(solution)/shard_map/kap,lcp->kalc/dot_general | solution.py:31
  117.3 0.0 all-reduce.3.cloned.1.call-update
  117.3 1.1 slice_bitcast_fusion
  118.4 0.1 copy.61
  118.5 70.4 %reduce-scatter.2.cloned.1.call-done = f32[64,16,128]{2,1,0:T(8,128)} async-done(((f32[512,16,128]{2,1,0:T(8,128)}), f32[64,16,128]{2,1,0:T(8,128)}) %reduce-scatter.2.cloned.1.call-update) | async-done | bytes 524304 | tf_op jit(solution)/shard_map/reduce_scatter | solution.py:25
  188.9 0.0 copy-done.1
  188.9 0.0 copy-start
  188.9 17.2 %convolution_bitcast_fusion.1 = f32[8,16,16]{1,2,0:T(8,128)S(1)} fusion(f32[8,16,8192]{2,1,0:T(8,128)} %param.6, f32[8192]{0:T(1024)S(1)} %copy-done.1, f32[64,16,128]{2,1,0:T(8,128)} %reduce-scatter.2.cloned.1.call-done), kind=kOutput, calls=%fused_computation.12 | convolution fusion | flops 201588736 | bytes 5283840 | tf_op jit(solution)/shard_map/kap,bp->kab/dot_general | solution.py:29
  206.1 0.0 copy-done
  206.1 1.0 convolution_bitcast_fusion.5
  207.1 41.0 %all-reduce = (f32[8,16,16]{1,2,0:T(8,128)S(1)}, f32[16,16]{0,1:T(8,128)S(1)}) all-reduce(f32[8,16,16]{1,2,0:T(8,128)S(1)} %convolution_bitcast_fusion.1, f32[16,16]{0,1:T(8,128)S(1)} %convolution_bitcast_fusion.5), channel_id=1, replica_groups=mesh['row'=8,'col'=4] {'row','col'}, use_global_device_ids=true, to_apply=%region_3.4 | all-reduce | flops 2304 | bytes 18432 | tf_op jit(solution)/shard_map/psum | solution.py:32
  248.1 14.4 %all-reduce.3.cloned.1.call-done = f32[8,16,8,16]{3,1,2,0:T(8,128)} async-done(((f32[8,16,8,16]{3,1,2,0:T(8,128)}), f32[8,16,8,16]{3,1,2,0:T(8,128)}) %all-reduce.3.cloned.1.call-update) | async-done | bytes 65552 | tf_op jit(solution)/shard_map/psum | solution.py:32
  262.5 1.4 convolution_bitcast_fusion.2
  263.9 0.2 convolution_bitcast_fusion.3
  264.1 0.2 fusion.11
  264.3 0.1 copy.40
  264.4 1.5 cholesky.16
  265.9 0.6 compare_reduce_fusion
  266.6 0.6 fusion.21
  267.2 1.2 custom-call.6
  268.5 0.7 copy.42
  269.1 0.7 copy.41
  269.9 6.7 %fusion.2 = f32[16,8192]{1,0:T(8,128)S(1)} fusion(f32[8,16,8192]{2,1,0:T(8,128)} %param.6, f32[8192]{0:T(1024)S(1)} %copy-done.1, f32[8,16,16]{1,2,0:T(8,128)S(1)} %get-tuple-element.12, f32[64,16,128]{2,1,0:T(8,128)S(1)} %copy-done), kind=kOutput, calls=%fused_computation.5 | convolution fusion | flops 201721856 | bytes 5808128 | tf_op jit(solution)/shard_map/kab,kap->bp/dot_general | solution.py:36
  276.6 1.4 fusion.18
  (5 shorter events, 0.1 us)
Async XLA Ops:
  8.0 22.4 %all-gather.2.cloned.1.call-start = ((), (), s32[]{:S(2)}) async-start(), calls=%async_computation.1 | async-start | bytes 1310720 | tf_op jit(solution)/shard_map/all_gather | solution.py:13
  9.8 179.0 %reduce-scatter.2.cloned.1.call-start = ((), (), s32[]{:S(2)}) async-start(), calls=%async_computation.2 | async-start | bytes 4718592 | tf_op jit(solution)/shard_map/reduce_scatter | solution.py:25
  99.0 89.8 %copy-start.1 = (f32[8192]{0:T(1024)S(1)}, f32[8192]{0:T(1024)}, u32[]{:S(2)}) copy-start(f32[8192]{0:T(1024)} %param.11) | copy-start | bytes 98308
  99.0 163.4 %all-reduce.3.cloned.1.call-start = ((), (), s32[]{:S(2)}) async-start(), calls=%async_computation.3 | async-start | bytes 1048576 | tf_op jit(solution)/shard_map/psum | solution.py:32
  188.9 17.2 %copy-start = (f32[64,16,128]{2,1,0:T(8,128)S(1)}, f32[64,16,128]{2,1,0:T(8,128)}, u32[]{:S(2)}) copy-start(f32[64,16,128]{2,1,0:T(8,128)} %reduce-scatter.2.cloned.1.call-done) | copy-start | bytes 1572868
Sparse Core Ops, SparseCore 0:
  10.9 19.4 all-gather.1
  99.1 89.6 reduce-scatter.1
Sparse Core Ops, SparseCore 1:
  117.4 145.0 all-reduce.2
where the time goes:
time: 288 us; the launch traced here: 285 us
  waiting for transfers between devices  103 us (36%)
  other arithmetic  57.3 us (20%)
  matrix products  53.1 us (18%)
  blocking collectives  41 us (14%)
  between operations  16.2 us (6%)
  local copies, waits for them, and re-layouts  15.1 us (5%)
    reduce_scatter x1, waiting for transfers between devices, local(): lax.psum_scatter(summed[:block_tiles], 'row', scatter_dimension=0, tiled=...  70.4 us
    scatter-add x1, other arithmetic, local(): jax.ops.segment_sum(products, segment_ids, num_segments=block_tiles + 1)  51.1 us
    psum x1, blocking collectives, local(): lax.psum((local_proj, local_self, local_basis), ('row', 'col'))  41 us
    dot_general x1, matrix products, local(): jnp.einsum('kap,lcp->kalc', basis_blocks, basis_blocks, precision=highest)  18 us
    all_gather x1, waiting for transfers between devices, local(): expanded = lax.all_gather(vector, 'col', axis=1, tiled=True)  17.7 us
    dot_general x1, matrix products, local(): jnp.einsum('kap,bp->kab', basis_blocks, image_rows, precision=highest)  17.2 us
    psum x1, waiting for transfers between devices, local(): lax.psum((local_proj, local_self, local_basis), ('row', 'col'))  14.4 us
    dot_general x1, matrix products, local(): jnp.einsum('stj,tji->tsi', gathered, values, preferred_element_type=jnp.f...  6.87 us
  transfers between devices with their start and end apart: 3, of which 3 were waited for; matrix products, arithmetic and copies ran while one was open for 14% of the time, Pallas kernels for 0%

commit v1 on v0

--- a/solution.py
+++ b/solution.py
@@ -2,6 +2,11 @@
 import jax.numpy as jnp
 from jax import lax
 from jax.sharding import PartitionSpec as P
+
+
+def one_after_other(array, inner_axis, outer_axis):
+    inner = lax.psum(array, inner_axis)
+    return lax.psum(inner, outer_axis)
 
 
 def local(basis_blocks, tile_values, tile_rows, tile_column, tile_count, diagonal):
@@ -29,7 +34,9 @@
     local_proj = jnp.einsum("kap,bp->kab", basis_blocks, image_rows, precision=highest)
     local_self = jnp.dot(image_rows, image_rows.T, precision=highest)
     local_basis = jnp.einsum("kap,lcp->kalc", basis_blocks, basis_blocks, precision=highest)
-    proj_sum, image_sum, basis_sum = lax.psum((local_proj, local_self, local_basis), ("row", "col"))
+    proj_sum, image_sum, basis_sum = one_after_other(
+        (local_proj, local_self, local_basis), "col", "row"
+    )
     coefficients = proj_sum / total_rows
     image_gram = image_sum / total_rows
     basis_gram = basis_sum / total_rows

time: 288 us -> 287 us (level)
  blocking collectives: 41 us -> 48.9 us
  waiting for transfers between devices: 103 us -> 98.1 us
    reduce_scatter x1, waiting for transfers between devices: 70.4 us -> 88.1 us  [local(): lax.psum_scatter(summed[:block_tiles], 'row', scatter_dimension=0, tiled=...]
    all_gather x1, waiting for transfers between devices: 17.7 us -> 1.06 us  [local(): expanded = lax.all_gather(vector, 'col', axis=1, tiled=True)]
    psum x1 -> x2, blocking collectives: 41 us -> 48.9 us  [the longest x1 37.5 us: one_after_other(): return lax.psum(inner, outer_axis)]
    psum x1 -> x2, waiting for transfers between devices: 14.4 us -> 8.87 us  [the longest x1 8.85 us: one_after_other(): return lax.psum(inner, outer_axis)]
  transfers between devices with their start and end apart: 3 -> 4, of which waited for: 3 -> 3; matrix products, arithmetic and copies ran while one was open for 14% -> 37% of each run, Pallas kernels for 0% -> 0%
where the time goes in v1:
time: 287 us; the launch traced here: 285 us
  waiting for transfers between devices  98.1 us (34%)
  other arithmetic  55.2 us (19%)
  matrix products  53.1 us (19%)
  blocking collectives  48.9 us (17%)
  local copies, waits for them, and re-layouts  15.1 us (5%)
  between operations  14.6 us (5%)
    reduce_scatter x1, waiting for transfers between devices, local(): lax.psum_scatter(summed[:block_tiles], 'row', scatter_dimension=0, tiled=...  88.1 us
    scatter-add x1, other arithmetic, local(): jax.ops.segment_sum(products, segment_ids, num_segments=block_tiles + 1)  51.1 us
    psum x1, blocking collectives, one_after_other(): return lax.psum(inner, outer_axis)  37.5 us
    dot_general x1, matrix products, local(): jnp.einsum('kap,lcp->kalc', basis_blocks, basis_blocks, precision=highest)  18 us
    dot_general x1, matrix products, local(): jnp.einsum('kap,bp->kab', basis_blocks, image_rows, precision=highest)  17.1 us
    psum x1, blocking collectives, one_after_other(): inner = lax.psum(array, inner_axis)  11.5 us
    psum x1, waiting for transfers between devices, one_after_other(): return lax.psum(inner, outer_axis)  8.85 us
    dot_general x1, matrix products, local(): jnp.einsum('stj,tji->tsi', gathered, values, preferred_element_type=jnp.f...  6.97 us
  transfers between devices with their start and end apart: 4, of which 3 were waited for; matrix products, arithmetic and copies ran while one was open for 37% of the time, Pallas kernels for 0%

profile of v1, /device:TPU:0, one launch (start us, length us, event | category | flops | bytes accessed | tf_op | source)
XLA Modules:
  0.0 285.4 jit_solution(2259027449141796488)
XLA Ops:
  7.2 0.0 all-gather.2.cloned.1.call-start
  7.2 1.8 bitcast_convert_fusion
  9.0 0.0 all-gather.2.cloned.1.call-update
  9.0 0.0 copy-start.2
  9.0 0.0 copy-start.3
  9.0 0.0 all-reduce.5.cloned.1.call-start
  9.1 18.0 %fusion.3 = f32[8,16,8,16]{3,1,2,0:T(8,128)} fusion(f32[8,16,8192]{2,1,0:T(8,128)} %param.6), kind=kOutput, calls=%fused_computation.6 | convolution fusion | flops 1610612736 | bytes 4259840 | tf_op jit(solution)/shard_map/kap,lcp->kalc/dot_general | solution.py:36
  27.1 0.0 all-reduce.5.cloned.1.call-update
  27.1 0.0 reduce-scatter.2.cloned.1.call-start
  27.2 0.0 copy-done.2
  27.9 0.0 copy-done.3
  27.9 1.1 all-gather.2.cloned.1.call-done
  29.0 1.4 copy_bitcast_fusion
  30.4 2.6 gather_fusion
  33.0 7.0 %fusion = f32[384,16,128]{2,1,0:T(8,128)S(1)} fusion(bf16[1,1,384,128,128]{4,3,2,1,0:T(8,128)(2,1)} %param.7, bf16[384,16,128]{2,1,0:T(8,128)(2,1)} %gather_fusion, pred[384]{0:T(512)(128)(4,1)S(1)} %compare_and_fusion), kind=kOutput, calls=%fused_computation.2 | convolution fusion | flops 202113024 | bytes 17301888 | tf_op jit(solution)/shard_map/stj,tji->tsi/dot_general | solution.py:26
  39.9 2.2 broadcast_in_dim.19
  42.2 51.1 %scatter_fusion = f32[513,16,128]{2,1,0:T(8,128)} fusion(f32[513,16,128]{2,1,0:T(8,128)} %broadcast_in_dim.19, s32[384]{0:T(512)S(1)} %fusion.23, f32[384,16,128]{2,1,0:T(8,128)S(1)} %fusion), kind=kCustom, calls=%fused_computation.1 | custom fusion | flops 786432 | bytes 9438720 | tf_op jit(solution)/shard_map/scatter-add | solution.py:29
  93.3 4.4 %slice.21 = f32[512,16,128]{2,1,0:T(8,128)} slice(f32[513,16,128]{2,1,0:T(8,128)} %scatter_fusion), slice={[0:512], [0:16], [0:128]} | slice | bytes 8388608 | tf_op jit(solution)/shard_map/slice | solution.py:30
  97.7 0.0 copy-start.1
  97.7 0.0 reduce-scatter.2.cloned.1.call-update
  97.7 0.2 all-reduce.7.cloned.1.call-start
  98.0 1.1 slice_bitcast_fusion
  99.0 0.1 copy.61
  99.2 0.0 all-reduce.5.cloned.1.call-done
  99.2 0.0 all-reduce.7.cloned.1.call-update
  99.2 88.1 %reduce-scatter.2.cloned.1.call-done = f32[64,16,128]{2,1,0:T(8,128)} async-done(((f32[512,16,128]{2,1,0:T(8,128)}), f32[64,16,128]{2,1,0:T(8,128)}) %reduce-scatter.2.cloned.1.call-update) | async-done | bytes 524304 | tf_op jit(solution)/shard_map/reduce_scatter | solution.py:30
  187.4 0.0 copy-done.1
  187.4 0.0 copy-start
  187.4 17.1 %convolution_bitcast_fusion.1 = f32[8,16,16]{1,2,0:T(8,128)S(1)} fusion(f32[8,16,8192]{2,1,0:T(8,128)} %param.6, f32[8192]{0:T(1024)S(1)} %copy-done.1, f32[64,16,128]{2,1,0:T(8,128)} %reduce-scatter.2.cloned.1.call-done), kind=kOutput, calls=%fused_computation.12 | convolution fusion | flops 201588736 | bytes 5283840 | tf_op jit(solution)/shard_map/kap,bp->kab/dot_general | solution.py:34
  204.5 0.0 copy-done
  204.5 1.0 convolution_bitcast_fusion.5
  205.5 11.5 %all-reduce.1 = (f32[8,16,16]{1,2,0:T(8,128)S(1)}, f32[16,16]{0,1:T(8,128)S(1)}) all-reduce(f32[8,16,16]{1,2,0:T(8,128)S(1)} %convolution_bitcast_fusion.1, f32[16,16]{0,1:T(8,128)S(1)} %convolution_bitcast_fusion.5), channel_id=1, replica_groups=mesh['row'=8,'col'=4] {'col'}, use_global_device_ids=true, to_apply=%region_4.5 | all-reduce | flops 2304 | bytes 18432 | tf_op jit(solution)/shard_map/psum | solution.py:8
  217.0 37.5 %all-reduce = (f32[8,16,16]{1,2,0:T(8,128)S(1)}, f32[16,16]{0,1:T(8,128)S(1)}) all-reduce(f32[8,16,16]{1,2,0:T(8,128)S(1)} %get-tuple-element.14, f32[16,16]{0,1:T(8,128)S(1)} %get-tuple-element.15), channel_id=1, replica_groups=mesh['row'=8,'col'=4] {'row'}, use_global_device_ids=true, to_apply=%region_5.6 | all-reduce | flops 2304 | bytes 18432 | tf_op jit(solution)/shard_map/psum | solution.py:9
  254.4 8.9 %all-reduce.7.cloned.1.call-done = f32[8,16,8,16]{3,1,2,0:T(8,128)} async-done(((f32[8,16,8,16]{3,1,2,0:T(8,128)}), f32[8,16,8,16]{3,1,2,0:T(8,128)}) %all-reduce.7.cloned.1.call-update) | async-done | bytes 65552 | tf_op jit(solution)/shard_map/psum | solution.py:9
  263.3 1.4 convolution_bitcast_fusion.2
  264.7 0.2 convolution_bitcast_fusion.3
  264.9 0.2 fusion.11
  265.1 0.1 copy.40
  265.2 1.5 cholesky.16
  266.7 0.6 compare_reduce_fusion
  267.4 0.6 fusion.21
  268.0 1.2 custom-call.6
  269.3 0.7 copy.42
  270.0 0.7 copy.41
  270.7 6.7 %fusion.2 = f32[16,8192]{1,0:T(8,128)S(1)} fusion(f32[8,16,8192]{2,1,0:T(8,128)} %param.6, f32[8192]{0:T(1024)S(1)} %copy-done.1, f32[8,16,16]{1,2,0:T(8,128)S(1)} %get-tuple-element.12, f32[64,16,128]{2,1,0:T(8,128)S(1)} %copy-done), kind=kOutput, calls=%fused_computation.5 | convolution fusion | flops 201721856 | bytes 5808128 | tf_op jit(solution)/shard_map/kab,kap->bp/dot_general | solution.py:43
  277.4 1.4 fusion.18
  (8 shorter events, 0.1 us)
Async XLA Ops:
  7.2 21.8 %all-gather.2.cloned.1.call-start = ((), (), s32[]{:S(2)}) async-start(), calls=%async_computation.1 | async-start | bytes 1310720 | tf_op jit(solution)/shard_map/all_gather | solution.py:18
  9.0 18.2 %copy-start.2 = (s32[1,1,384]{2,1,0:T(1,128)S(1)}, s32[1,1,384]{2,1,0:T(1,128)}, u32[]{:S(2)}) copy-start(s32[1,1,384]{2,1,0:T(1,128)} %param.9) | copy-start | bytes 4612
  9.0 18.9 %copy-start.3 = (s32[1,1,384]{2,1,0:T(1,128)S(1)}, s32[1,1,384]{2,1,0:T(1,128)}, u32[]{:S(2)}) copy-start(s32[1,1,384]{2,1,0:T(1,128)} %param.8) | copy-start | bytes 4612
  9.0 90.1 %all-reduce.5.cloned.1.call-start = ((), (), s32[]{:S(2)}) async-start(), calls=%async_computation.3 | async-start | bytes 1048576 | tf_op jit(solution)/shard_map/psum | solution.py:8
  27.1 160.2 %reduce-scatter.2.cloned.1.call-start = ((), (), s32[]{:S(2)}) async-start(), calls=%async_computation.2 | async-start | bytes 4718592 | tf_op jit(solution)/shard_map/reduce_scatter | solution.py:30
  97.7 89.7 %copy-start.1 = (f32[8192]{0:T(1024)S(1)}, f32[8192]{0:T(1024)}, u32[]{:S(2)}) copy-start(f32[8192]{0:T(1024)} %param.11) | copy-start | bytes 98308
  97.7 165.6 %all-reduce.7.cloned.1.call-start = ((), (), s32[]{:S(2)}) async-start(), calls=%async_computation.4 | async-start | bytes 1048576 | tf_op jit(solution)/shard_map/psum | solution.py:9
  187.4 17.1 %copy-start = (f32[64,16,128]{2,1,0:T(8,128)S(1)}, f32[64,16,128]{2,1,0:T(8,128)}, u32[]{:S(2)}) copy-start(f32[64,16,128]{2,1,0:T(8,128)} %reduce-scatter.2.cloned.1.call-done) | copy-start | bytes 1572868
Sparse Core Ops, SparseCore 0:
  9.5 19.4 all-gather.1
  31.9 33.3 all-reduce.4
  97.9 89.4 reduce-scatter.1
  190.6 72.6 all-reduce.6
